TPU v7x, 512 devices: a 8x2x16 block of a 8x8x16 slice. The times are simulated.
512 devices in a mesh: groups: 2 (over y), docs: 16 (over z), mp: 8 (over x), sub: 2 (over core).
Axes of the slice: x: 8, y: 2, z: 16, core: 2. Of those that a mesh axis runs over, the one named last changes fastest.
The devices are a block of a 8x8x16 slice.
Arguments:
- embeddings: bfloat16 [65536, 1024], P(('groups', 'docs', 'mp', 'sub')), parts along dimension 0, may hold values from -6 to 6
- owner_shard: int32 [65536, 1], P(('groups', 'docs', 'mp', 'sub')), parts along dimension 0, may hold values from 0 to 15; in each aligned block of 128 rows (0 to 127, 128 to 255, ...) at most 16 rows name the same one
- query_local: int32 [65536], P(('groups', 'docs', 'mp', 'sub')), parts along dimension 0, may hold values from 0 to 1
- labels: int32 [65536], P(('groups', 'docs', 'mp', 'sub')), parts along dimension 0, may hold values from 0 to 4
- w_first: bfloat16 [1024, 1024], replicated, may hold values from -0.1875 to 0.1875
- w_second: float32 [1024], replicated, may hold values from -0.1875 to 0.1875
Outputs:
- emb_grad: bfloat16 [65536, 1024], P(('groups', 'docs', 'mp', 'sub')), parts along dimension 0
- w_first_grad: float32 [2048, 1024], P(('groups', 'mp', 'sub')), parts along dimension 0
- w_second_grad: float32 [2048], P('groups'), parts along dimension 0
There are 2 independent parts, one for each index of `groups`. A program takes and returns all parts, laid end to end along the dimension named above; an argument that names none is the same for every part. Nothing has to cross between parts.
Inputs may be any that keep to these rules, and one draw needn't show every extreme that they name: `owner_shard`: among the 128 rows of one document shard no owner appears more than 16 times, and some owner appears exactly 16 times.
All inputs are finite; a program needn't handle non-finite values.
Results may differ from a plain program's by a relative error of at most 0.017.
Values may be sent and summed in bfloat16 or wider, within the bound.
No kernel may reach another device: no remote copies, remote signals or barrier semaphores. Data moves between devices by JAX's collectives and lax.ppermute only.
A program may use at most 64 MiB of HBM per device.

v0:
```python
import functools

import jax
import jax.numpy as jnp
from jax import lax
from jax.experimental import pallas as pl
from jax.experimental.pallas import tpu as pltpu
from jax.sharding import PartitionSpec as P


LANES = 128


def whole(*shape_and_type):
    return jax.ShapeDtypeStruct(*shape_and_type)


def on_chip(x):
    return pltpu.with_memory_space_constraint(x, pltpu.VMEM)


def vmem_specs(count):
    return [pl.BlockSpec(memory_space=pltpu.VMEM)] * count


def score_kernel(capacity, emb_ref, w1_ref, w2_ref, owner_ref, query_ref, label_ref, sent_ref, slot_ref):
    rows = emb_ref.shape[0]
    halves = sent_ref.shape[1] // 4
    along = lax.broadcasted_iota(jnp.int32, (rows, rows), 1)
    down = lax.broadcasted_iota(jnp.int32, (rows, rows), 0)

    def column(row):
        return jnp.sum(jnp.where(along == down, row, 0), axis=1, keepdims=True)

    owner = owner_ref[...]
    owner_column = column(owner)
    earlier = jnp.where((owner_column == owner) & (along < down), 1, 0)
    slot = owner_column * capacity + jnp.sum(earlier, axis=1, keepdims=True)
    slot_ref[...] = slot
    mark = column(query_ref[...] + 1).astype(jnp.float32)
    label = column(label_ref[...]).astype(jnp.float32)

    pre_act = jnp.dot(emb_ref[...], w1_ref[...], preferred_element_type=jnp.float32)
    hidden = pre_act * jax.nn.sigmoid(pre_act)
    score = jnp.sum(hidden * w2_ref[...], axis=1, keepdims=True)

    lane = lax.broadcasted_iota(jnp.int32, (rows, LANES), 1)
    sent_ref[...] = jnp.zeros_like(sent_ref)
    for h in range(halves):
        here = slot == lane + h * LANES
        for place, value in enumerate((score, mark, label)):
            row = jnp.sum(jnp.where(here, value, 0.0), axis=0, keepdims=True)
            for target in range(sent_ref.shape[0]):
                sent_ref[target, place * halves + h : place * halves + h + 1, :] = row


def within_groups(x, capacity):
    lane = lax.broadcasted_iota(jnp.int32, x.shape, 1)
    out = [x]
    step = capacity // 2
    while step:
        upper = (lane & step) != 0
        spread = []
        for y in out:
            spread.append(jnp.where(upper, pltpu.roll(y, step, 1), y))
            spread.append(jnp.where(upper, y, pltpu.roll(y, LANES - step, 1)))
        out = spread
        step //= 2
    return out


def group_sum(x, capacity):
    lane = lax.broadcasted_iota(jnp.int32, x.shape, 1)
    step = capacity // 2
    while step:
        upper = (lane & step) != 0
        x = x + jnp.where(upper, pltpu.roll(x, step, 1), pltpu.roll(x, LANES - step, 1))
        step //= 2
    return x


def lambda_kernel(
    capacity, place_ref, got_ref, slot_ref, spread_ref, column_ref,
    score_by, mark_by, key_by, disc_by, row_scratch,
):
    sources = got_ref.shape[0]
    halves = got_ref.shape[1] // 4
    me = place_ref[0]
    rows = slot_ref.shape[0]
    source = lax.broadcasted_iota(jnp.int32, (sources, LANES), 0)
    lane = lax.broadcasted_iota(jnp.int32, (sources, LANES), 1)
    position = (source * capacity + lane % capacity).astype(jnp.float32)
    slots = float(sources * capacity)
    trip = 2 * sources
    lane_of_row = lax.broadcasted_iota(jnp.int32, (rows, LANES), 1)
    lambda_column = jnp.zeros((rows, 1), jnp.float32)
    for h in range(halves):
        half_score = got_ref[:, h, :] * 0.5
        mark = got_ref[:, halves + h, :]
        label = got_ref[:, 2 * halves + h, :]
        key = (label + 8.0 * mark) * slots - position
        counts = []
        for query in range(2):
            here = jnp.sum(jnp.where(mark == query + 1.0, 1.0, 0.0), axis=0, keepdims=True)
            counts.append(group_sum(jnp.broadcast_to(here, (8, LANES)), capacity)[:1, :])
        first, other = counts
        fellows = jnp.where(mark == 1.0, first, jnp.where(mark == 2.0, other, slots - first - other))
        above = jnp.where(mark == 1.0, other, jnp.where(mark == 2.0, 0.0, first + other))
        for ref, value in ((score_by, half_score), (mark_by, mark), (key_by, key)):
            for c, spread in enumerate(within_groups(value, capacity)):
                ref[c * sources : (c + 1) * sources, :] = spread

        def rank_step(step, sums):
            soft, ideal = sums
            base = pl.multiple_of(step * trip, trip)
            score_rows = score_by[pl.ds(base, trip), :]
            mark_rows = mark_by[pl.ds(base, trip), :]
            key_rows = key_by[pl.ds(base, trip), :]
            for r in range(trip):
                same = mark_rows[r : r + 1, :] == mark
                tilt = jnp.tanh(score_rows[r : r + 1, :] - half_score)
                soft = soft + jnp.where(same, tilt, 0.0)
                ideal = ideal + jnp.where(key_rows[r : r + 1, :] > key, 1.0, 0.0)
            return soft, ideal

        nothing = jnp.zeros((sources, LANES), jnp.float32)
        soft, ideal = lax.fori_loop(0, capacity * sources // trip, rank_step, (nothing, nothing))
        discount = 1.0 / jnp.log2(2.0 + (0.5 * (soft + fellows) - 0.5))
        gain = jnp.exp2(label) - 1.0
        term = gain / jnp.log2(2.0 + (ideal - above))
        for c, spread in enumerate(within_groups(discount, capacity)):
            disc_by[c * sources : (c + 1) * sources, :] = spread

        for place, value in enumerate((half_score, mark, gain, discount)):
            row_scratch[place * sources : (place + 1) * sources, :] = value
        own_score, own_mark, own_gain, own_disc = (
            row_scratch[pl.ds(place * sources + me, 1), :] for place in range(4)
        )
        ideal_sum = jnp.zeros((1, LANES), jnp.float32)
        for query in range(2):
            asked = query + 1.0
            per_lane = jnp.sum(jnp.where(mark == asked, term, 0.0), axis=0, keepdims=True)
            spread = group_sum(jnp.broadcast_to(per_lane, (8, LANES)), capacity)[:1, :]
            ideal_sum = jnp.where(own_mark == asked, spread, ideal_sum)
        inv_ideal = jnp.where(ideal_sum > 0.0, 1.0 / jnp.where(ideal_sum > 0.0, ideal_sum, 1.0), 0.0)

        total = jnp.zeros((sources, LANES), jnp.float32)
        for c in range(capacity):
            at = slice(c * sources, (c + 1) * sources)
            their_label = jnp.ceil(key_by[at, :] * (1.0 / slots)) - 8.0 * mark_by[at, :]
            their_gain = jnp.exp2(their_label) - 1.0
            gain_gap = own_gain - their_gain
            gap = 2.0 * (score_by[at, :] - own_score)
            pull = jax.nn.sigmoid(jnp.where(gain_gap > 0.0, gap, -gap))
            pair = -gain_gap * jnp.abs(own_disc - disc_by[at, :]) * pull
            total = total + jnp.where(mark_by[at, :] == own_mark, pair, 0.0)
        lambda_row = jnp.sum(total, axis=0, keepdims=True) * inv_ideal
        here = slot_ref[...] == lane_of_row + h * LANES
        lambda_column = lambda_column + jnp.sum(
            jnp.where(here, lambda_row, 0.0), axis=1, keepdims=True
        )

    column_ref[...] = lambda_column
    along = lax.broadcasted_iota(jnp.int32, (rows, rows), 1)
    down = lax.broadcasted_iota(jnp.int32, (rows, rows), 0)
    row = jnp.sum(jnp.where(along == down, lambda_column, 0.0), axis=0, keepdims=True)
    spread_ref[...] = jnp.broadcast_to(row[None], spread_ref.shape)


def slope_kernel(count, place_ref, w1_ref, w2_ref, *refs):
    emb_refs, out_ref = refs[:count], refs[count]
    units = w1_ref.shape[1]
    wide = out_ref.shape[2] - 2 * units
    mine = pl.ds(pl.multiple_of(place_ref[1] // 2 * wide, LANES), wide)
    for i, emb_ref in enumerate(emb_refs):
        pre_act = jnp.dot(emb_ref[...], w1_ref[...], preferred_element_type=jnp.float32)
        gate = jax.nn.sigmoid(pre_act)
        out_ref[i, :, units : 2 * units] = (pre_act * gate).astype(jnp.bfloat16)
        slope = gate * (1.0 + pre_act * (1.0 - gate))
        out_ref[i, :, :units] = (w2_ref[...] * slope).astype(jnp.bfloat16)
        out_ref[i, :, 2 * units :] = emb_ref[:, mine]


def slopes(place, w_first, w2_row, blocks, wide):
    rows, units = blocks[0].shape[0], w_first.shape[1]
    count = len(blocks)
    return pl.pallas_call(
        functools.partial(slope_kernel, count),
        out_shape=pltpu.VMEM((count, rows, 2 * units + wide), jnp.bfloat16),
        in_specs=[pl.BlockSpec(memory_space=pltpu.SMEM)] + vmem_specs(2 + count),
        out_specs=vmem_specs(1)[0],
        name="slopes",
    )(place, w_first, w2_row, *blocks)


def product_kernel(offsets, units, place_ref, lambda_ref, ready_ref, sent_ref):
    members, rows = lambda_ref.shape[0], lambda_ref.shape[2]
    my_member = place_ref[1] // 2
    along = lax.broadcasted_iota(jnp.int32, (rows, rows), 1)
    down = lax.broadcasted_iota(jnp.int32, (rows, rows), 0)
    total, second = None, None
    for i, offset in enumerate(offsets):
        block = lambda_ref[lax.rem(my_member + offset, members)]
        column = jnp.sum(jnp.where(along == down, block[:1], 0.0), axis=1, keepdims=True)
        part = (ready_ref[i, :, 2 * units :].astype(jnp.float32) * column).astype(jnp.bfloat16)
        product = lax.dot_general(
            part, ready_ref[i, :, :units], (((0,), (0,)), ((), ())),
            preferred_element_type=jnp.float32,
        )
        high = block.astype(jnp.bfloat16)
        low = (block - high.astype(jnp.float32)).astype(jnp.bfloat16)
        hidden = ready_ref[i, :, units : 2 * units]
        summed = jnp.dot(high, hidden, preferred_element_type=jnp.float32) + jnp.dot(
            low, hidden, preferred_element_type=jnp.float32
        )
        total = product if total is None else total + product
        second = summed if second is None else second + summed
    targets = sent_ref.shape[0]
    part_rows = total.shape[0] // targets
    columns = total.shape[1] // LANES
    rounded, second = total.astype(jnp.bfloat16), second.astype(jnp.bfloat16)
    for target in range(targets):
        for k in range(columns):
            at = slice(k * LANES, (k + 1) * LANES)
            sent_ref[target, k * part_rows : (k + 1) * part_rows, :] = rounded[
                target * part_rows : (target + 1) * part_rows, at
            ]
            row = part_rows * columns + k
            sent_ref[target, row : row + 1, :] = second[:1, at]


def sent_to_all(x, axis):
    count = lax.axis_size(axis)
    return lax.all_to_all(jnp.broadcast_to(x[None], (count, *x.shape)), axis, 0, 0, tiled=True)


def parity_blocks(block):
    lanes, subs = lax.axis_size("mp"), lax.axis_size("sub")

    def moved(x, by):
        return lax.ppermute(x, "mp", [(i, (i + by) % lanes) for i in range(lanes)])

    back, on = moved(block, 2), moved(block, -2)
    both_ways = [
        (i * subs + s, (i + (2 if s == 0 else -2)) % lanes * subs + s)
        for i in range(lanes)
        for s in range(subs)
    ]
    passed = jnp.where(lax.axis_index("sub") == 0, back, on)
    across = lax.ppermute(passed, ("mp", "sub"), both_ways)
    return back, on, across


def on_device(embeddings, owner_shard, query_local, labels, w_first, w_second):
    docs, lanes, subs = (lax.axis_size(axis) for axis in ("docs", "mp", "sub"))
    rows, width = embeddings.shape
    units = w_first.shape[1]
    capacity = 2 * rows // docs
    halves = docs * capacity // LANES
    w2_row = w_second.reshape(1, units)
    place = jnp.stack([lax.axis_index(axis) for axis in ("docs", "mp", "sub")]).astype(jnp.int32)
    back, on, across = parity_blocks(embeddings)
    members = lanes // 2
    sent, slot = pl.pallas_call(
        functools.partial(score_kernel, capacity),
        out_shape=(
            whole((docs, 4 * halves, LANES), jnp.float32),
            whole((rows, 1), jnp.int32),
        ),
        in_specs=vmem_specs(6),
        out_specs=tuple(vmem_specs(2)),
        name="score",
    )(
        embeddings, w_first, w2_row,
        owner_shard.reshape(1, rows), query_local.reshape(1, rows), labels.reshape(1, rows),
    )
    got = lax.all_to_all(sent, "docs", 0, 0, tiled=True)
    spread, lambda_column = pl.pallas_call(
        functools.partial(lambda_kernel, capacity),
        out_shape=(whole((members, 8, rows), jnp.float32), whole((rows, 1), jnp.float32)),
        in_specs=[pl.BlockSpec(memory_space=pltpu.SMEM)] + vmem_specs(2),
        out_specs=tuple(vmem_specs(2)),
        scratch_shapes=[pltpu.VMEM((docs * capacity, LANES), jnp.float32)] * 4
        + [pltpu.VMEM((4 * docs, LANES), jnp.float32)],
        name="lambdas",
    )(place, on_chip(got), slot)
    parities = [list(range(parity, lanes, 2)) for parity in range(2)]
    all_lambdas = lax.all_to_all(
        spread, "mp", 0, 0, axis_index_groups=parities, tiled=True
    )

    part_rows = width // (lanes * subs)
    targets = 2 * subs
    wide = targets * part_rows
    columns = units // LANES
    prepared = slopes(place, w_first, w2_row, [embeddings, back, on, across], wide)
    own_grad = lax.dot_general(
        prepared[0, :, :units], w_first, (((1,), (1,)), ((), ())), preferred_element_type=jnp.float32
    )
    emb_grad = (lambda_column * own_grad).astype(jnp.bfloat16)
    all_lambdas, emb_grad = lax.optimization_barrier((all_lambdas, emb_grad))
    offsets = (0, members - 1, 1, 2)
    sent = pl.pallas_call(
        functools.partial(product_kernel, offsets, units),
        out_shape=pltpu.VMEM((targets, (part_rows + 1) * columns, LANES), jnp.bfloat16),
        in_specs=[pl.BlockSpec(memory_space=pltpu.SMEM)] + vmem_specs(2),
        out_specs=vmem_specs(1)[0],
        name="product",
    )(place, on_chip(all_lambdas), on_chip(prepared))
    cells = [list(range(i, i + targets)) for i in range(0, lanes * subs, targets)]
    arrived = lax.all_to_all(
        sent, ("mp", "sub"), 0, 0, axis_index_groups=cells, tiled=True
    )
    line_sum = arrived.astype(jnp.float32).sum(axis=0).astype(jnp.bfloat16)
    first_rows = part_rows * columns
    tiles = line_sum[:first_rows].reshape(docs, first_rows // docs, LANES)
    second = jnp.broadcast_to(line_sum[first_rows:][None], (docs, columns, LANES))
    arrived = lax.all_to_all(jnp.concatenate([tiles, second], axis=1), "docs", 0, 0, tiled=True)
    shard_sum = arrived.astype(jnp.float32).sum(axis=0)
    spread = sent_to_all(shard_sum[: first_rows // docs].astype(jnp.bfloat16), "docs")
    shard_sum, spread = lax.optimization_barrier((shard_sum, spread))
    w_second_grad = shard_sum[first_rows // docs :].reshape(units)
    w_first_grad = (
        spread.reshape(columns, part_rows, LANES).transpose(1, 0, 2).reshape(part_rows, units)
    ).astype(jnp.float32)
    return (emb_grad, w_first_grad, w_second_grad)


def solution(mesh):
    split = ("groups", "docs", "mp", "sub")
    return jax.shard_map(
        on_device,
        mesh=mesh,
        in_specs=(P(split, None), P(split, None), P(split), P(split), P(), P()),
        out_specs=(P(split, None), P(("groups", "mp", "sub"), None), P("groups")),
        check_vma=False,
    )
```

profile of v0, /device:TPU:80, one launch (start us, length us, event | category | flops | bytes accessed | tf_op | source)
XLA Modules:
  0.0 155.7 jit_solution(2909437528160444171)
XLA Ops:
  0.6 4.6 %collective-permute-start = (bf16[128,1024]{1,0:T(8,128)(2,1)}, bf16[128,1024]{1,0:T(8,128)(2,1)S(1)}, u32[]{:S(2)}, u32[]{:S(2)}) collective-permute-start(bf16[128,1024]{1,0:T(8,128)(2,1)} %refs_0_.1), channel_id=1, source_target_pairs={{0,4},{2,6},{4,8},{6,10},{8,12},{10,14},{12,0},{14,2},{1,5},{3,7},... | collective-permute-start | bytes 786440 | tf_op jit(solution)/shard_map/ppermute | solution.py:241
  5.3 3.8 %collective-permute-start.1 = (bf16[128,1024]{1,0:T(8,128)(2,1)}, bf16[128,1024]{1,0:T(8,128)(2,1)S(1)}, u32[]{:S(2)}, u32[]{:S(2)}) collective-permute-start(bf16[128,1024]{1,0:T(8,128)(2,1)} %refs_0_.1), channel_id=1, source_target_pairs={{0,12},{2,14},{4,0},{6,2},{8,4},{10,6},{12,8},{14,10},{1,13},{3,15... | collective-permute-start | bytes 786440 | tf_op jit(solution)/shard_map/ppermute | solution.py:241
  9.1 7.5 %collective-permute-done.refs_1_ = bf16[128,1024]{1,0:T(8,128)(2,1)S(1)} collective-permute-done((bf16[128,1024]{1,0:T(8,128)(2,1)}, bf16[128,1024]{1,0:T(8,128)(2,1)S(1)}, u32[]{:S(2)}, u32[]{:S(2)}) %collective-permute-start) | collective-permute-done | bytes 262176 | tf_op jit(solution)/shard_map/ppermute | solution.py:241
  16.6 6.4 %collective-permute-done.1.refs_2_ = bf16[128,1024]{1,0:T(8,128)(2,1)S(1)} collective-permute-done((bf16[128,1024]{1,0:T(8,128)(2,1)}, bf16[128,1024]{1,0:T(8,128)(2,1)S(1)}, u32[]{:S(2)}, u32[]{:S(2)}) %collective-permute-start.1) | collective-permute-done | bytes 262176 | tf_op jit(solution)/shard_map/ppermute | solution.py:241
  23.1 5.2 %collective-permute-start.2 = (bf16[128,1024]{1,0:T(8,128)(2,1)S(1)}, bf16[128,1024]{1,0:T(8,128)(2,1)S(1)}, u32[]{:S(2)}, u32[]{:S(2)}) collective-permute-start(bf16[128,1024]{1,0:T(8,128)(2,1)S(1)} %broadcast_select_fusion), channel_id=1, source_target_pairs={{0,4},{1,13},{2,6},{3,15},{4,8},{5,1},{6,10},{7,3},{8,12},{9,5},{1... | collective-permute-start | bytes 786440 | tf_op jit(solution)/shard_map/ppermute | solution.py:250
  28.3 2.8 %score.1 = (f32[16,8,128]{2,1,0:T(8,128)}, s32[128,1]{1,0:T(8,128)}) custom-call(bf16[128,1024]{1,0:T(8,128)(2,1)} %refs_0_.1, bf16[1024,1024]{1,0:T(8,128)(2,1)} %w1_ref.3, f32[1,1024]{1,0:T(1,128)} %bitcast.28, s32[1,128]{1,0:T(1,128)} %bitcast.30, s32[1,128]{1,0:T(1,128)} %bitcast.31, s32[1,128]{1,0:T(1,128)} %bitcast.32), custom_call_target="tpu_custom_call" | custom-call | tf_op jit(solution)/shard_map/score/pallas_call | solution.py:264
  31.1 43.7 %all-to-all-start = ((f32[16,8,128]{2,1,0:T(8,128)}), f32[16,8,128]{2,1,0:T(8,128)S(1)}, u32[]{:S(2)}, u32[]{:S(2)}) async-start(f32[16,8,128]{2,1,0:T(8,128)} %get-tuple-element.11), calls=%async_computation | async-start | bytes 131072 | tf_op jit(solution)/shard_map/all_to_all | solution.py:277
  74.8 0.6 pad_add_fusion.place_ref
  75.4 12.1 %all-to-all-done.got_ref = f32[16,8,128]{2,1,0:T(8,128)S(1)} async-done(((f32[16,8,128]{2,1,0:T(8,128)}), f32[16,8,128]{2,1,0:T(8,128)S(1)}, u32[]{:S(2)}, u32[]{:S(2)}) %all-to-all-start) | async-done | bytes 65568 | tf_op jit(solution)/shard_map/all_to_all | solution.py:277
  87.5 4.1 %lambdas.1 = (f32[4,8,128]{2,1,0:T(8,128)}, f32[128,1]{1,0:T(8,128)}) custom-call(s32[3]{0:T(128)} %pad_add_fusion.place_ref, f32[16,8,128]{2,1,0:T(8,128)S(1)} %all-to-all-done.got_ref, s32[128,1]{1,0:T(8,128)} %get-tuple-element.12.slot_ref), custom_call_target="tpu_custom_call" | custom-call | tf_op jit(solution)/shard_map/lambdas/pallas_call | solution.py:278
  91.6 3.3 %all-to-all-start.1 = ((f32[4,8,128]{2,1,0:T(8,128)}), f32[4,8,128]{2,1,0:T(8,128)S(1)}, u32[]{:S(2)}, u32[]{:S(2)}) async-start(f32[4,8,128]{2,1,0:T(8,128)} %get-tuple-element.13), calls=%async_computation.1 | async-start | bytes 32768 | tf_op jit(solution)/shard_map/all_to_all | solution.py:288
  94.9 0.9 reduce.1
  95.9 0.0 collective-permute-done.2.refs_3_
  95.9 0.7 copy-done.2
  96.6 3.5 %slopes.1.ready_ref = bf16[4,128,2304]{2,1,0:T(8,128)(2,1)S(1)} custom-call(s32[3]{0:T(128)} %pad_add_fusion.place_ref, bf16[1024,1024]{1,0:T(8,128)(2,1)} %w1_ref.3, f32[1,1024]{1,0:T(1,128)} %bitcast.29, bf16[128,1024]{1,0:T(8,128)(2,1)} %refs_0_.1, bf16[128,1024]{1,0:T(8,128)(2,1)} %copy-done, bf16[128,1024]{1,0:T(8,128)(2,1)} %copy-done.1, ...), custom_call_target="tpu_custom_call" | custom-call | tf_op jit(solution)/shard_map/slopes/pallas_call | solution.py:187
  100.1 3.1 %fusion = bf16[128,1024]{1,0:T(8,128)(2,1)} fusion(bf16[1024,1024]{1,0:T(8,128)(2,1)} %w1_ref.3, bf16[4,128,2304]{2,1,0:T(8,128)(2,1)S(1)} %slopes.1.ready_ref, f32[128]{0:T(128)S(1)} %reduce.1), kind=kOutput, calls=%fused_computation.1 | convolution fusion | flops 268697600 | bytes 2621952 | tf_op jit(solution)/shard_map/dot_general | solution.py:297
  103.2 0.0 all-to-all-done.1.lambda_ref
  103.2 1.7 %product.1 = bf16[4,520,128]{2,1,0:T(8,128)(2,1)S(1)} custom-call(s32[3]{0:T(128)} %pad_add_fusion.place_ref, f32[4,8,128]{2,1,0:T(8,128)S(1)} %all-to-all-done.1.lambda_ref, bf16[4,128,2304]{2,1,0:T(8,128)(2,1)S(1)} %slopes.1.ready_ref), custom_call_target="tpu_custom_call" | custom-call | tf_op jit(solution)/shard_map/product/pallas_call | solution.py:303
  104.9 11.4 %all_to_all.25 = bf16[4,520,128]{2,1,0:T(8,128)(2,1)S(1)} all-to-all(bf16[4,520,128]{2,1,0:T(8,128)(2,1)S(1)} %product.1), channel_id=1, replica_groups={{0,1,2,3},{4,5,6,7},{8,9,10,11},{12,13,14,15},{16,17,18,19},{20,21,22,2..., dimensions={0} | all-to-all | bytes 1064960 | tf_op jit(solution)/shard_map/all_to_all | solution.py:311
  116.3 0.1 reduce_sum.21
  116.4 18.7 %all_to_all.26 = bf16[16,40,128]{2,1,0:T(8,128)(2,1)S(1)} all-to-all(bf16[16,40,128]{2,1,0:T(8,128)(2,1)S(1)} %pad_maximum_fusion), channel_id=1, replica_groups=mesh['groups'=2,'docs'=16,'mp'=8,'sub'=2] {'docs'}, dimensions={0} | all-to-all | bytes 327680 | tf_op jit(solution)/shard_map/all_to_all | solution.py:318
  135.1 19.3 %all_to_all.27 = bf16[16,32,128]{2,1,0:T(8,128)(2,1)S(1)} all-to-all(bf16[16,32,128]{2,1,0:T(8,128)(2,1)S(1)} %broadcast_in_dim.5), channel_id=1, replica_groups=mesh['groups'=2,'docs'=16,'mp'=8,'sub'=2] {'docs'}, dimensions={0} | all-to-all | bytes 262144 | tf_op jit(solution)/shard_map/all_to_all | solution.py:234
  154.4 0.6 slice_bitcast_fusion.2
  155.0 0.7 copy_bitcast_fusion
  (13 shorter events, 0.1 us)
Async XLA Ops:
  0.6 16.0 %collective-permute-start = (bf16[128,1024]{1,0:T(8,128)(2,1)}, bf16[128,1024]{1,0:T(8,128)(2,1)S(1)}, u32[]{:S(2)}, u32[]{:S(2)}) collective-permute-start(bf16[128,1024]{1,0:T(8,128)(2,1)} %refs_0_.1), channel_id=1, source_target_pairs={{0,4},{2,6},{4,8},{6,10},{8,12},{10,14},{12,0},{14,2},{1,5},{3,7},... | collective-permute-start | bytes 786440 | tf_op jit(solution)/shard_map/ppermute | solution.py:241
  5.3 17.8 %collective-permute-start.1 = (bf16[128,1024]{1,0:T(8,128)(2,1)}, bf16[128,1024]{1,0:T(8,128)(2,1)S(1)}, u32[]{:S(2)}, u32[]{:S(2)}) collective-permute-start(bf16[128,1024]{1,0:T(8,128)(2,1)} %refs_0_.1), channel_id=1, source_target_pairs={{0,12},{2,14},{4,0},{6,2},{8,4},{10,6},{12,8},{14,10},{1,13},{3,15... | collective-permute-start | bytes 786440 | tf_op jit(solution)/shard_map/ppermute | solution.py:241
  16.6 79.2 %copy-start = (bf16[128,1024]{1,0:T(8,128)(2,1)}, bf16[128,1024]{1,0:T(8,128)(2,1)S(1)}, u32[]{:S(2)}) copy-start(bf16[128,1024]{1,0:T(8,128)(2,1)S(1)} %collective-permute-done.refs_1_) | copy-start | bytes 786436
  23.0 72.9 %copy-start.1 = (bf16[128,1024]{1,0:T(8,128)(2,1)}, bf16[128,1024]{1,0:T(8,128)(2,1)S(1)}, u32[]{:S(2)}) copy-start(bf16[128,1024]{1,0:T(8,128)(2,1)S(1)} %collective-permute-done.1.refs_2_) | copy-start | bytes 786436
  23.1 72.8 %collective-permute-start.2 = (bf16[128,1024]{1,0:T(8,128)(2,1)S(1)}, bf16[128,1024]{1,0:T(8,128)(2,1)S(1)}, u32[]{:S(2)}, u32[]{:S(2)}) collective-permute-start(bf16[128,1024]{1,0:T(8,128)(2,1)S(1)} %broadcast_select_fusion), channel_id=1, source_target_pairs={{0,4},{1,13},{2,6},{3,15},{4,8},{5,1},{6,10},{7,3},{8,12},{9,5},{1... | collective-permute-start | bytes 786440 | tf_op jit(solution)/shard_map/ppermute | solution.py:250
  31.1 56.4 %all-to-all-start = ((f32[16,8,128]{2,1,0:T(8,128)}), f32[16,8,128]{2,1,0:T(8,128)S(1)}, u32[]{:S(2)}, u32[]{:S(2)}) async-start(f32[16,8,128]{2,1,0:T(8,128)} %get-tuple-element.11), calls=%async_computation | async-start | bytes 131072 | tf_op jit(solution)/shard_map/all_to_all | solution.py:277
  91.6 11.6 %all-to-all-start.1 = ((f32[4,8,128]{2,1,0:T(8,128)}), f32[4,8,128]{2,1,0:T(8,128)S(1)}, u32[]{:S(2)}, u32[]{:S(2)}) async-start(f32[4,8,128]{2,1,0:T(8,128)} %get-tuple-element.13), calls=%async_computation.1 | async-start | bytes 32768 | tf_op jit(solution)/shard_map/all_to_all | solution.py:288
  95.9 0.7 copy-start.2
where the time goes:
time: 157 us; the launch traced here: 156 us
  starting transfers between devices  60.7 us (39%)
  blocking collectives  49.3 us (31%)
  waiting for transfers between devices  26.1 us (17%)
  Pallas kernels  12.1 us (8%)
  matrix products  3.13 us (2%)
  other arithmetic  2.41 us (2%)
    all_to_all x1, starting transfers between devices, on_device(): got = lax.all_to_all(sent, 'docs', 0, 0, tiled=True)  43.7 us
    all_to_all x1, blocking collectives, sent_to_all(): lax.all_to_all(jnp.broadcast_to(x[None], (count, *x.shape)), axis, 0, 0,...  19.3 us
    all_to_all x1, blocking collectives, on_device(): lax.all_to_all(jnp.concatenate([tiles, second], axis=1), 'docs', 0, 0, ti...  18.7 us
    ppermute x2, waiting for transfers between devices, moved(): return lax.ppermute(x, 'mp', [(i, (i + by) % lanes) for i in range(lanes)])  13.9 us
    all_to_all x1, waiting for transfers between devices, on_device(): got = lax.all_to_all(sent, 'docs', 0, 0, tiled=True)  12.1 us
    all_to_all x1, blocking collectives, on_device(): lax.all_to_all(sent, ('mp', 'sub'), 0, 0, axis_index_groups=cells, tiled=...  11.4 us
    ppermute x2, starting transfers between devices, moved(): return lax.ppermute(x, 'mp', [(i, (i + by) % lanes) for i in range(lanes)])  8.45 us
    ppermute x1, starting transfers between devices, parity_blocks(): across = lax.ppermute(passed, ('mp', 'sub'), both_ways)  5.2 us
  transfers between devices with their start and end apart: 5, of which 3 were waited for; matrix products, arithmetic and copies ran while one was open for 3% of the time, Pallas kernels for 7%

commit v1 on v0

--- a/solution.py
+++ b/solution.py
@@ -91,7 +91,7 @@
     lane = lax.broadcasted_iota(jnp.int32, (sources, LANES), 1)
     position = (source * capacity + lane % capacity).astype(jnp.float32)
     slots = float(sources * capacity)
-    trip = 2 * sources
+    trip = 4 * sources
     lane_of_row = lax.broadcasted_iota(jnp.int32, (rows, LANES), 1)
     lambda_column = jnp.zeros((rows, 1), jnp.float32)
     for h in range(halves):
@@ -294,11 +294,6 @@
     wide = targets * part_rows
     columns = units // LANES
     prepared = slopes(place, w_first, w2_row, [embeddings, back, on, across], wide)
-    own_grad = lax.dot_general(
-        prepared[0, :, :units], w_first, (((1,), (1,)), ((), ())), preferred_element_type=jnp.float32
-    )
-    emb_grad = (lambda_column * own_grad).astype(jnp.bfloat16)
-    all_lambdas, emb_grad = lax.optimization_barrier((all_lambdas, emb_grad))
     offsets = (0, members - 1, 1, 2)
     sent = pl.pallas_call(
         functools.partial(product_kernel, offsets, units),
@@ -317,9 +312,13 @@
     second = jnp.broadcast_to(line_sum[first_rows:][None], (docs, columns, LANES))
     arrived = lax.all_to_all(jnp.concatenate([tiles, second], axis=1), "docs", 0, 0, tiled=True)
     shard_sum = arrived.astype(jnp.float32).sum(axis=0)
+    lambda_column, shard_sum = lax.optimization_barrier((lambda_column, shard_sum))
+    own_grad = lax.dot_general(
+        prepared[0, :, :units], w_first, (((1,), (1,)), ((), ())), preferred_element_type=jnp.float32
+    )
+    emb_grad = (lambda_column * own_grad).astype(jnp.bfloat16)
+    w_second_grad = shard_sum[first_rows // docs :].reshape(units)
     spread = sent_to_all(shard_sum[: first_rows // docs].astype(jnp.bfloat16), "docs")
-    shard_sum, spread = lax.optimization_barrier((shard_sum, spread))
-    w_second_grad = shard_sum[first_rows // docs :].reshape(units)
     w_first_grad = (
         spread.reshape(columns, part_rows, LANES).transpose(1, 0, 2).reshape(part_rows, units)
     ).astype(jnp.float32)

time: 157 us -> 140 us (0.89)
  blocking collectives: 49.3 us -> 29.3 us
  starting transfers between devices: 60.7 us -> 68.6 us
  waiting for transfers between devices: 26.1 us -> 22.1 us
    all_to_all x1 -> x0, blocking collectives: 19.3 us -> none  [sent_to_all(): lax.all_to_all(jnp.broadcast_to(x[None], (count, *x.shape)), axis, 0, 0,...]
    ppermute x2, waiting for transfers between devices: 13.9 us -> 0.01 us  [moved(): return lax.ppermute(x, 'mp', [(i, (i + by) % lanes) for i in range(lanes)])]
    all_to_all x0 -> x1, waiting for transfers between devices: none -> 10.8 us  [sent_to_all(): lax.all_to_all(jnp.broadcast_to(x[None], (count, *x.shape)), axis, 0, 0,...]
    all_to_all x0 -> x1, starting transfers between devices: none -> 5.5 us  [sent_to_all(): lax.all_to_all(jnp.broadcast_to(x[None], (count, *x.shape)), axis, 0, 0,...]
    all_to_all x1, waiting for transfers between devices: 12.1 us -> 7.8 us  [on_device(): got = lax.all_to_all(sent, 'docs', 0, 0, tiled=True)]
    all_to_all x1, starting transfers between devices: 3.34 us -> 6.99 us  [on_device(): lax.all_to_all(spread, 'mp', 0, 0, axis_index_groups=parities, tiled=True)]
    all_to_all x1, waiting for transfers between devices: 0.01 us -> 3.54 us  [on_device(): lax.all_to_all(spread, 'mp', 0, 0, axis_index_groups=parities, tiled=True)]
  transfers between devices with their start and end apart: 5 -> 6, of which waited for: 3 -> 3; matrix products, arithmetic and copies ran while one was open for 3% -> 3% of each run, Pallas kernels for 7% -> 7%
where the time goes in v1:
time: 140 us
  starting transfers between devices  68.6 us (49%)
  blocking collectives  29.3 us (21%)
  waiting for transfers between devices  22.1 us (16%)
  Pallas kernels  12 us (9%)
  matrix products  3.12 us (2%)
  local copies, waits for them, and re-layouts  2.01 us (1%)
  other arithmetic  1.63 us (1%)
    all_to_all x1, starting transfers between devices, on_device(): got = lax.all_to_all(sent, 'docs', 0, 0, tiled=True)  43.7 us
    all_to_all x1, blocking collectives, on_device(): lax.all_to_all(jnp.concatenate([tiles, second], axis=1), 'docs', 0, 0, ti...  17.8 us
    all_to_all x1, blocking collectives, on_device(): lax.all_to_all(sent, ('mp', 'sub'), 0, 0, axis_index_groups=cells, tiled=...  11.5 us
    all_to_all x1, waiting for transfers between devices, sent_to_all(): lax.all_to_all(jnp.broadcast_to(x[None], (count, *x.shape)), axis, 0, 0,...  10.8 us
    ppermute x2, starting transfers between devices, moved(): return lax.ppermute(x, 'mp', [(i, (i + by) % lanes) for i in range(lanes)])  8.45 us
    all_to_all x1, waiting for transfers between devices, on_device(): got = lax.all_to_all(sent, 'docs', 0, 0, tiled=True)  7.8 us
    all_to_all x1, starting transfers between devices, on_device(): lax.all_to_all(spread, 'mp', 0, 0, axis_index_groups=parities, tiled=True)  6.99 us
    all_to_all x1, starting transfers between devices, sent_to_all(): lax.all_to_all(jnp.broadcast_to(x[None], (count, *x.shape)), axis, 0, 0,...  5.5 us
  transfers between devices with their start and end apart: 6, of which 3 were waited for; matrix products, arithmetic and copies ran while one was open for 3% of the time, Pallas kernels for 7%

profile of v1, /device:TPU:80, one launch (start us, length us, event | category | flops | bytes accessed | tf_op | source)
XLA Modules:
  0.0 139.7 jit_solution(17925282215662634794)
XLA Ops:
  0.6 4.6 %collective-permute-start = (bf16[128,1024]{1,0:T(8,128)(2,1)}, bf16[128,1024]{1,0:T(8,128)(2,1)S(1)}, u32[]{:S(2)}, u32[]{:S(2)}) collective-permute-start(bf16[128,1024]{1,0:T(8,128)(2,1)} %refs_0_.1), channel_id=1, source_target_pairs={{0,4},{2,6},{4,8},{6,10},{8,12},{10,14},{12,0},{14,2},{1,5},{3,7},... | collective-permute-start | bytes 786440 | tf_op jit(solution)/shard_map/ppermute | solution.py:241
  5.3 3.8 %collective-permute-start.1 = (bf16[128,1024]{1,0:T(8,128)(2,1)}, bf16[128,1024]{1,0:T(8,128)(2,1)S(1)}, u32[]{:S(2)}, u32[]{:S(2)}) collective-permute-start(bf16[128,1024]{1,0:T(8,128)(2,1)} %refs_0_.1), channel_id=1, source_target_pairs={{0,12},{2,14},{4,0},{6,2},{8,4},{10,6},{12,8},{14,10},{1,13},{3,15... | collective-permute-start | bytes 786440 | tf_op jit(solution)/shard_map/ppermute | solution.py:241
  9.1 2.8 %score.1 = (f32[16,8,128]{2,1,0:T(8,128)}, s32[128,1]{1,0:T(8,128)}) custom-call(bf16[128,1024]{1,0:T(8,128)(2,1)} %refs_0_.1, bf16[1024,1024]{1,0:T(8,128)(2,1)} %w1_ref.3, f32[1,1024]{1,0:T(1,128)} %bitcast.28, s32[1,128]{1,0:T(1,128)} %bitcast.30, s32[1,128]{1,0:T(1,128)} %bitcast.31, s32[1,128]{1,0:T(1,128)} %bitcast.32), custom_call_target="tpu_custom_call" | custom-call | tf_op jit(solution)/shard_map/score/pallas_call | solution.py:264
  11.9 43.7 %all-to-all-start = ((f32[16,8,128]{2,1,0:T(8,128)}), f32[16,8,128]{2,1,0:T(8,128)S(1)}, u32[]{:S(2)}, u32[]{:S(2)}) async-start(f32[16,8,128]{2,1,0:T(8,128)} %get-tuple-element.9), calls=%async_computation | async-start | bytes 131072 | tf_op jit(solution)/shard_map/all_to_all | solution.py:277
  55.6 0.0 copy-start
  55.7 4.0 %collective-permute-start.2 = (bf16[128,1024]{1,0:T(8,128)(2,1)S(1)}, bf16[128,1024]{1,0:T(8,128)(2,1)S(1)}, u32[]{:S(2)}, u32[]{:S(2)}) collective-permute-start(bf16[128,1024]{1,0:T(8,128)(2,1)S(1)} %broadcast_select_fusion), channel_id=1, source_target_pairs={{0,4},{1,13},{2,6},{3,15},{4,8},{5,1},{6,10},{7,3},{8,12},{9,5},{1... | collective-permute-start | bytes 786440 | tf_op jit(solution)/shard_map/ppermute | solution.py:250
  59.7 0.7 pad_add_fusion.place_ref
  60.3 7.8 %all-to-all-done.got_ref = f32[16,8,128]{2,1,0:T(8,128)S(1)} async-done(((f32[16,8,128]{2,1,0:T(8,128)}), f32[16,8,128]{2,1,0:T(8,128)S(1)}, u32[]{:S(2)}, u32[]{:S(2)}) %all-to-all-start) | async-done | bytes 65568 | tf_op jit(solution)/shard_map/all_to_all | solution.py:277
  68.1 4.0 %lambdas.1 = (f32[4,8,128]{2,1,0:T(8,128)}, f32[128,1]{1,0:T(8,128)}) custom-call(s32[3]{0:T(128)} %pad_add_fusion.place_ref, f32[16,8,128]{2,1,0:T(8,128)S(1)} %all-to-all-done.got_ref, s32[128,1]{1,0:T(8,128)} %get-tuple-element.10.slot_ref), custom_call_target="tpu_custom_call" | custom-call | tf_op jit(solution)/shard_map/lambdas/pallas_call | solution.py:278
  72.1 7.0 %all-to-all-start.1 = ((f32[4,8,128]{2,1,0:T(8,128)}), f32[4,8,128]{2,1,0:T(8,128)S(1)}, u32[]{:S(2)}, u32[]{:S(2)}) async-start(f32[4,8,128]{2,1,0:T(8,128)} %get-tuple-element.12), calls=%async_computation.1 | async-start | bytes 32768 | tf_op jit(solution)/shard_map/all_to_all | solution.py:288
  79.2 0.7 copy-done.2
  79.8 3.5 %slopes.1.ready_ref = bf16[4,128,2304]{2,1,0:T(8,128)(2,1)S(1)} custom-call(s32[3]{0:T(128)} %pad_add_fusion.place_ref, bf16[1024,1024]{1,0:T(8,128)(2,1)} %w1_ref.3, f32[1,1024]{1,0:T(1,128)} %bitcast.29, bf16[128,1024]{1,0:T(8,128)(2,1)} %refs_0_.1, bf16[128,1024]{1,0:T(8,128)(2,1)} %copy-done, bf16[128,1024]{1,0:T(8,128)(2,1)} %copy-done.1, ...), custom_call_target="tpu_custom_call" | custom-call | tf_op jit(solution)/shard_map/slopes/pallas_call | solution.py:187
  83.4 3.5 %all-to-all-done.1.lambda_ref = f32[4,8,128]{2,1,0:T(8,128)S(1)} async-done(((f32[4,8,128]{2,1,0:T(8,128)}), f32[4,8,128]{2,1,0:T(8,128)S(1)}, u32[]{:S(2)}, u32[]{:S(2)}) %all-to-all-start.1) | async-done | bytes 16416 | tf_op jit(solution)/shard_map/all_to_all | solution.py:288
  86.9 1.7 %product.1 = bf16[4,520,128]{2,1,0:T(8,128)(2,1)S(1)} custom-call(s32[3]{0:T(128)} %pad_add_fusion.place_ref, f32[4,8,128]{2,1,0:T(8,128)S(1)} %all-to-all-done.1.lambda_ref, bf16[4,128,2304]{2,1,0:T(8,128)(2,1)S(1)} %slopes.1.ready_ref), custom_call_target="tpu_custom_call" | custom-call | tf_op jit(solution)/shard_map/product/pallas_call | solution.py:298
  88.6 11.5 %all_to_all.25 = bf16[4,520,128]{2,1,0:T(8,128)(2,1)S(1)} all-to-all(bf16[4,520,128]{2,1,0:T(8,128)(2,1)S(1)} %product.1), channel_id=1, replica_groups={{0,1,2,3},{4,5,6,7},{8,9,10,11},{12,13,14,15},{16,17,18,19},{20,21,22,2..., dimensions={0} | all-to-all | bytes 1064960 | tf_op jit(solution)/shard_map/all_to_all | solution.py:306
  100.1 0.1 reduce_sum.21
  100.2 17.8 %all_to_all.26 = bf16[16,40,128]{2,1,0:T(8,128)(2,1)S(1)} all-to-all(bf16[16,40,128]{2,1,0:T(8,128)(2,1)S(1)} %pad_maximum_fusion), channel_id=1, replica_groups=mesh['groups'=2,'docs'=16,'mp'=8,'sub'=2] {'docs'}, dimensions={0} | all-to-all | bytes 327680 | tf_op jit(solution)/shard_map/all_to_all | solution.py:313
  118.1 0.7 broadcast_in_dim.5
  118.8 5.5 %all-to-all-start.4 = ((bf16[16,32,128]{2,1,0:T(8,128)(2,1)}), bf16[16,32,128]{2,1,0:T(8,128)(2,1)S(1)}, u32[]{:S(2)}, u32[]{:S(2)}) async-start(bf16[16,32,128]{2,1,0:T(8,128)(2,1)} %broadcast_in_dim.5), calls=%async_computation.4 | async-start | bytes 262144 | tf_op jit(solution)/shard_map/all_to_all | solution.py:234
  124.3 0.1 reduce.1
  124.4 0.6 slice_bitcast_fusion.2
  125.0 3.1 %fusion = bf16[128,1024]{1,0:T(8,128)(2,1)} fusion(bf16[1024,1024]{1,0:T(8,128)(2,1)} %w1_ref.3, bf16[4,128,2304]{2,1,0:T(8,128)(2,1)S(1)} %slopes.1.ready_ref, f32[128]{0:T(128)S(1)} %reduce.1), kind=kOutput, calls=%fused_computation.1 | convolution fusion | flops 268697600 | bytes 2621952 | tf_op jit(solution)/shard_map/dot_general | solution.py:316
  128.2 10.8 %all-to-all-done.4 = bf16[16,32,128]{2,1,0:T(8,128)(2,1)S(1)} async-done(((bf16[16,32,128]{2,1,0:T(8,128)(2,1)}), bf16[16,32,128]{2,1,0:T(8,128)(2,1)S(1)}, u32[]{:S(2)}, u32[]{:S(2)}) %all-to-all-start.4) | async-done | bytes 131104 | tf_op jit(solution)/shard_map/all_to_all | solution.py:234
  138.9 0.7 copy_bitcast_fusion
  (16 shorter events, 0.1 us)
Async XLA Ops:
  0.6 55.0 %collective-permute-start = (bf16[128,1024]{1,0:T(8,128)(2,1)}, bf16[128,1024]{1,0:T(8,128)(2,1)S(1)}, u32[]{:S(2)}, u32[]{:S(2)}) collective-permute-start(bf16[128,1024]{1,0:T(8,128)(2,1)} %refs_0_.1), channel_id=1, source_target_pairs={{0,4},{2,6},{4,8},{6,10},{8,12},{10,14},{12,0},{14,2},{1,5},{3,7},... | collective-permute-start | bytes 786440 | tf_op jit(solution)/shard_map/ppermute | solution.py:241
  5.3 50.3 %collective-permute-start.1 = (bf16[128,1024]{1,0:T(8,128)(2,1)}, bf16[128,1024]{1,0:T(8,128)(2,1)S(1)}, u32[]{:S(2)}, u32[]{:S(2)}) collective-permute-start(bf16[128,1024]{1,0:T(8,128)(2,1)} %refs_0_.1), channel_id=1, source_target_pairs={{0,12},{2,14},{4,0},{6,2},{8,4},{10,6},{12,8},{14,10},{1,13},{3,15... | collective-permute-start | bytes 786440 | tf_op jit(solution)/shard_map/ppermute | solution.py:241
  11.9 56.2 %all-to-all-start = ((f32[16,8,128]{2,1,0:T(8,128)}), f32[16,8,128]{2,1,0:T(8,128)S(1)}, u32[]{:S(2)}, u32[]{:S(2)}) async-start(f32[16,8,128]{2,1,0:T(8,128)} %get-tuple-element.9), calls=%async_computation | async-start | bytes 131072 | tf_op jit(solution)/shard_map/all_to_all | solution.py:277
  55.6 23.5 %copy-start = (bf16[128,1024]{1,0:T(8,128)(2,1)}, bf16[128,1024]{1,0:T(8,128)(2,1)S(1)}, u32[]{:S(2)}) copy-start(bf16[128,1024]{1,0:T(8,128)(2,1)S(1)} %collective-permute-done.refs_1_) | copy-start | bytes 786436
  55.6 23.5 %copy-start.1 = (bf16[128,1024]{1,0:T(8,128)(2,1)}, bf16[128,1024]{1,0:T(8,128)(2,1)S(1)}, u32[]{:S(2)}) copy-start(bf16[128,1024]{1,0:T(8,128)(2,1)S(1)} %collective-permute-done.1.refs_2_) | copy-start | bytes 786436
  55.7 23.5 %collective-permute-start.2 = (bf16[128,1024]{1,0:T(8,128)(2,1)S(1)}, bf16[128,1024]{1,0:T(8,128)(2,1)S(1)}, u32[]{:S(2)}, u32[]{:S(2)}) collective-permute-start(bf16[128,1024]{1,0:T(8,128)(2,1)S(1)} %broadcast_select_fusion), channel_id=1, source_target_pairs={{0,4},{1,13},{2,6},{3,15},{4,8},{5,1},{6,10},{7,3},{8,12},{9,5},{1... | collective-permute-start | bytes 786440 | tf_op jit(solution)/shard_map/ppermute | solution.py:250
  72.1 14.8 %all-to-all-start.1 = ((f32[4,8,128]{2,1,0:T(8,128)}), f32[4,8,128]{2,1,0:T(8,128)S(1)}, u32[]{:S(2)}, u32[]{:S(2)}) async-start(f32[4,8,128]{2,1,0:T(8,128)} %get-tuple-element.12), calls=%async_computation.1 | async-start | bytes 32768 | tf_op jit(solution)/shard_map/all_to_all | solution.py:288
  79.1 0.7 copy-start.2
  88.6 35.7 %copy-start.3 = (f32[128,1]{1,0:T(8,128)S(1)}, f32[128,1]{1,0:T(8,128)}, u32[]{:S(2)}) copy-start(f32[128,1]{1,0:T(8,128)} %get-tuple-element.13) | copy-start | bytes 1540
  118.8 20.1 %all-to-all-start.4 = ((bf16[16,32,128]{2,1,0:T(8,128)(2,1)}), bf16[16,32,128]{2,1,0:T(8,128)(2,1)S(1)}, u32[]{:S(2)}, u32[]{:S(2)}) async-start(bf16[16,32,128]{2,1,0:T(8,128)(2,1)} %broadcast_in_dim.5), calls=%async_computation.4 | async-start | bytes 262144 | tf_op jit(solution)/shard_map/all_to_all | solution.py:234
